TPU v7x, 32 devices: a whole 2x2x4 slice. The times are simulated.
32 devices in a mesh: days: 4 (over y, x), space: 8 (over z, core).
Axes of the slice: x: 2, y: 2, z: 4, core: 2. Of those that a mesh axis runs over, the one named last changes fastest.
Arguments:
- fields: bfloat16 [640, 32, 1440], P('days', 'space')
- month_label: int32 [640], P('days'), may hold values from 0 to 11, as said below
- row_index: int32 [32], P('space'), may hold values from 0 to 31
- area_table: float32 [32], replicated, may hold values from 0.05 to 1
- basis: bfloat16 [64, 32, 1440], P(None, 'space'), may hold values from -6 to 6
Outputs:
- eofs: float32 [64, 32, 1440], P(None, 'space')
- pcs: float32 [640, 64], P('days')
Inputs may be any that keep to these rules, and one draw needn't show every extreme that they name: `month_label`: each day's label differs from floor(12 * day / 640) by at most one; the first day with a given value of floor(12 * day / 640) carries exactly that value; every month labels at least one day.
All inputs are finite; a program needn't handle non-finite values.
Results may differ from a plain program's by a relative error of at most 0.0003.
Values sent between devices are 32-bit elements; how exact they have to be, the bound alone decides.
A program may use at most 64 MiB of HBM per device.

v0:
```python
import jax
import jax.numpy as jnp
from jax import lax
from jax.sharding import PartitionSpec as P

ITERS = 2
HIGH = lax.Precision.HIGHEST


def solve_lower(lower, cover):
    shape = cover.shape
    solved = lax.linalg.triangular_solve(
        lower, cover.reshape(shape[0], -1), left_side=True, lower=True
    )
    return solved.reshape(shape)


def self_gram(cover):
    return jnp.einsum("klc,jlc->kj", cover, cover, precision=HIGH)


def local(fields, month_label, row_index, area_table, basis):
    months = jnp.arange(12, dtype=jnp.int32)
    onehot = (month_label[None, :] == months[:, None]).astype(jnp.bfloat16)
    sums = jnp.einsum("md,dlc->mlc", onehot, fields, preferred_element_type=jnp.float32)
    counts = jnp.sum(onehot.astype(jnp.float32), axis=1)
    sums, counts = lax.psum((sums, counts), "days")
    climate = sums / counts[:, None, None]
    seasonal = jnp.einsum("md,mlc->dlc", onehot.astype(jnp.float32), climate, precision=HIGH)
    table_hot = (
        row_index[:, None] == jnp.arange(area_table.shape[0], dtype=jnp.int32)[None, :]
    ).astype(jnp.float32)
    scale = jnp.sqrt(jnp.dot(table_hot, area_table, precision=HIGH))
    weighted = (fields.astype(jnp.float32) - seasonal) * scale[None, :, None]
    days_total = fields.shape[0] * lax.axis_size("days")
    partial_pcs = jnp.einsum("dlc,klc->dk", weighted, basis.astype(jnp.float32), precision=HIGH)
    pcs = lax.psum(partial_pcs, "space")
    eofs = basis.astype(jnp.float32)
    for step_count in range(ITERS):
        partial_cover = jnp.einsum("dk,dlc->klc", pcs, weighted, precision=HIGH) / days_total
        cover = lax.psum(partial_cover, "days")
        partial_gram = self_gram(cover)
        partial_raw = jnp.einsum("dlc,klc->dk", weighted, cover, precision=HIGH)
        gram, raw_pcs = lax.psum((partial_gram, partial_raw), "space")
        lower = jnp.linalg.cholesky(gram)
        eofs = solve_lower(lower, cover)
        pcs = lax.linalg.triangular_solve(
            lower, raw_pcs, left_side=False, lower=True, transpose_a=True
        )
    return (eofs, pcs)


def solution(mesh):
    placed = (P("days", "space", None), P("days"), P("space"), P(), P(None, "space", None))
    return jax.shard_map(
        local,
        mesh=mesh,
        in_specs=placed,
        out_specs=(P(None, "space", None), P("days", None)),
        check_vma=False,
    )
```

profile of v0, /device:TPU:0, one launch (start us, length us, event | category | flops | bytes accessed | tf_op | source)
XLA Modules:
  0.0 343.0 jit_solution(18154794807191105921)
XLA Ops:
  7.3 3.1 fusion
  10.6 11.5 %psum.64 = f32[12]{0:T(128)S(1)} all-reduce(f32[12]{0:T(128)S(1)} %convert_reduce_fusion), channel_id=1, replica_groups=mesh['days'=4,'space'=8] {'days'}, use_global_device_ids=true, to_apply=%region_2.0 | all-reduce | flops 12 | bytes 96 | tf_op jit(solution)/shard_map/psum | solution.py:27
  22.2 36.2 %all-reduce.6.cloned.1.call-done = f32[12,4,1440]{2,0,1:T(8,128)} async-done(((f32[12,4,1440]{2,0,1:T(8,128)}), f32[12,4,1440]{2,0,1:T(8,128)}) %all-reduce.6.cloned.1.call-update) | async-done | bytes 276496 | tf_op jit(solution)/shard_map/psum | solution.py:27
  58.4 3.2 subtract_multiply_fusion
  61.6 1.9 copy-done.1
  63.5 2.4 convolution_bitcast_fusion.4
  65.9 28.5 %psum.65 = f32[160,64]{0,1:T(8,128)S(1)} all-reduce(f32[160,64]{0,1:T(8,128)S(1)} %convolution_bitcast_fusion.4), channel_id=1, replica_groups=mesh['days'=4,'space'=8] {'space'}, use_global_device_ids=true, to_apply=%region_3.0 | all-reduce | flops 10240 | bytes 81920 | tf_op jit(solution)/shard_map/psum | solution.py:37
  94.4 5.4 %convolution_multiply_fusion.1 = f32[64,4,1440]{2,0,1:T(8,128)} fusion(f32[160,4,1440]{2,0,1:T(8,128)} %copy-done.1, f32[160,64]{0,1:T(8,128)S(1)} %psum.65), kind=kOutput, calls=%fused_computation.2 | convolution fusion | flops 708157440 | bytes 5201920 | tf_op jit(solution)/shard_map/dk,dlc->klc/dot_general | solution.py:40
  100.1 57.9 %all-reduce.8.cloned.1.call-done = f32[64,4,1440]{2,0,1:T(8,128)} async-done(((f32[64,4,1440]{2,0,1:T(8,128)}), f32[64,4,1440]{2,0,1:T(8,128)}) %all-reduce.8.cloned.1.call-update) | async-done | bytes 1474576 | tf_op jit(solution)/shard_map/psum | solution.py:41
  157.9 3.5 %convolution_bitcast_fusion.6 = f32[64,64]{0,1:T(8,128)S(1)} fusion(f32[64,4,1440]{2,0,1:T(8,128)} %all-reduce.8.cloned.1.call-done), kind=kOutput, calls=%fused_computation.13 | convolution fusion | flops 283115520 | bytes 1490944 | tf_op jit(solution)/shard_map/klc,jlc->kj/dot_general | solution.py:19
  161.4 5.3 %convolution_bitcast_fusion.1 = f32[160,64]{1,0:T(8,128)S(1)} fusion(f32[160,4,1440]{2,0,1:T(8,128)} %copy-done.1, f32[64,4,1440]{2,0,1:T(8,128)S(1)} %copy-done.3), kind=kOutput, calls=%fused_computation.8 | convolution fusion | flops 707788800 | bytes 5201920 | tf_op jit(solution)/shard_map/dlc,klc->dk/dot_general | solution.py:43
  166.7 29.8 %all-reduce.1 = (f32[160,64]{1,0:T(8,128)S(1)}, f32[64,64]{0,1:T(8,128)S(1)}) all-reduce(f32[160,64]{1,0:T(8,128)S(1)} %convolution_bitcast_fusion.1, f32[64,64]{0,1:T(8,128)S(1)} %convolution_bitcast_fusion.6), channel_id=1, replica_groups=mesh['days'=4,'space'=8] {'space'}, use_global_device_ids=true, to_apply=%region_8.0 | all-reduce | flops 14336 | bytes 114688 | tf_op jit(solution)/shard_map/psum | solution.py:44
  196.7 5.8 %cholesky.44 = f32[64,64]{1,0:T(8,128)S(1)} custom-call(f32[64,64]{1,0:T(8,128)S(1)} %fusion.15), custom_call_target="Cholesky" | custom-call | tf_op jit(solution)/shard_map/jit(cholesky)/cholesky | solution.py:45
  202.5 0.6 compare_reduce_fusion.1
  203.2 0.7 fusion.9
  203.8 4.9 %custom-call.10 = f32[1,64,64]{1,2,0:T(8,128)S(1)} custom-call(f32[1,64,64]{2,1,0:T(8,128)S(1)} %fusion.9), custom_call_target="InvertDiagBlocksLowerTriangular" | custom-call | tf_op jit(solution)/shard_map/triangular_solve/custom-call.0 | solution.py:47
  208.8 0.3 convolution_bitcast_fusion.3
  209.1 5.4 %convolution_multiply_fusion = f32[64,4,1440]{2,0,1:T(8,128)} fusion(f32[160,64,1]{0,1,2:T(8,128)S(1)} %convolution_bitcast_fusion.3, f32[160,4,1440]{2,0,1:T(8,128)} %copy-done.1), kind=kOutput, calls=%fused_computation.1 | convolution fusion | flops 708157440 | bytes 5201920 | tf_op jit(solution)/shard_map/dk,dlc->klc/dot_general | solution.py:40
  214.5 58.1 %all-reduce.10.cloned.1.call-done = f32[64,4,1440]{2,0,1:T(8,128)} async-done(((f32[64,4,1440]{2,0,1:T(8,128)}), f32[64,4,1440]{2,0,1:T(8,128)}) %all-reduce.10.cloned.1.call-update) | async-done | bytes 1474576 | tf_op jit(solution)/shard_map/psum | solution.py:41
  272.6 3.6 %copy.19 = f32[64,4,1440]{2,1,0:T(4,128)} copy(f32[64,4,1440]{2,0,1:T(8,128)} %all-reduce.10.cloned.1.call-done) | data formatting | bytes 2949120 | tf_op jit(solution)/shard_map/psum | solution.py:41
  276.2 3.3 reshape.27
  279.5 5.3 %convolution_bitcast_fusion = f32[160,64]{1,0:T(8,128)S(1)} fusion(f32[160,4,1440]{2,0,1:T(8,128)} %copy-done.1, f32[64,4,1440]{2,0,1:T(8,128)S(1)} %copy-done.2), kind=kOutput, calls=%fused_computation.7 | convolution fusion | flops 707788800 | bytes 5201920 | tf_op jit(solution)/shard_map/dlc,klc->dk/dot_general | solution.py:43
  284.8 1.4 convolution_bitcast_fusion.5
  286.2 30.2 %all-reduce = (f32[64,64]{0,1:T(8,128)S(1)}, f32[160,64]{1,0:T(8,128)S(1)}) all-reduce(f32[64,64]{0,1:T(8,128)S(1)} %convolution_bitcast_fusion.5, f32[160,64]{1,0:T(8,128)S(1)} %convolution_bitcast_fusion), channel_id=1, replica_groups=mesh['days'=4,'space'=8] {'space'}, use_global_device_ids=true, to_apply=%region_10.13 | all-reduce | flops 14336 | bytes 114688 | tf_op jit(solution)/shard_map/psum | solution.py:44
  316.5 5.8 %cholesky.55 = f32[64,64]{1,0:T(8,128)S(1)} custom-call(f32[64,64]{1,0:T(8,128)S(1)} %fusion.13), custom_call_target="Cholesky" | custom-call | tf_op jit(solution)/shard_map/jit(cholesky)/cholesky | solution.py:45
  322.4 0.6 compare_reduce_fusion
  323.1 0.7 fusion.10
  323.7 4.9 %custom-call.8 = f32[1,64,64]{1,2,0:T(8,128)S(1)} custom-call(f32[1,64,64]{2,1,0:T(8,128)S(1)} %fusion.10), custom_call_target="InvertDiagBlocksLowerTriangular" | custom-call | tf_op jit(solution)/shard_map/triangular_solve | solution.py:12
  328.6 2.9 triangular_solve.34
  331.5 0.9 convolution_bitcast_fusion.2
  332.5 1.9 fusion.2
  334.4 2.2 copy.22
  (29 shorter events, 0.9 us)
Async XLA Ops:
  7.2 56.3 %copy-start = (bf16[64,4,1440]{2,1,0:T(4,128)(2,1)S(1)}, bf16[64,4,1440]{2,1,0:T(4,128)(2,1)}, u32[]{:S(2)}) copy-start(bf16[64,4,1440]{2,1,0:T(4,128)(2,1)} %param.12) | copy-start | bytes 2211844
  7.2 3.3 copy-start.5
  7.2 51.2 %copy-start.4 = (bf16[160,4,1440]{2,1,0:T(4,128)(2,1)S(1)}, bf16[160,4,1440]{2,1,0:T(4,128)(2,1)}, u32[]{:S(2)}) copy-start(bf16[160,4,1440]{2,1,0:T(4,128)(2,1)} %param.8) | copy-start | bytes 5529604
  7.2 14.8 %copy-start.7 = (f32[32]{0:T(128)S(1)}, f32[32]{0:T(128)}, u32[]{:S(2)}) copy-start(f32[32]{0:T(128)} %param.11) | copy-start | bytes 388
  7.2 14.8 %copy-start.6 = (s32[4]{0:T(128)S(1)}, s32[4]{0:T(128)}, u32[]{:S(2)}) copy-start(s32[4]{0:T(128)} %param.10) | copy-start | bytes 52
  7.2 51.2 %all-reduce.6.cloned.1.call-start = ((), (), s32[]{:S(2)}) async-start(), calls=%async_computation | async-start | bytes 786432 | tf_op jit(solution)/shard_map/psum | solution.py:27
  10.4 147.5 %all-reduce.8.cloned.1.call-start = ((), (), s32[]{:S(2)}) async-start(), calls=%async_computation.1 | async-start | bytes 3145728 | tf_op jit(solution)/shard_map/psum | solution.py:41
  61.6 1.9 copy-start.1
  99.8 172.8 %all-reduce.10.cloned.1.call-start = ((), (), s32[]{:S(2)}) async-start(), calls=%async_computation.2 | async-start | bytes 3145728 | tf_op jit(solution)/shard_map/psum | solution.py:41
  157.9 3.5 %copy-start.3 = (f32[64,4,1440]{2,0,1:T(8,128)S(1)}, f32[64,4,1440]{2,0,1:T(8,128)}, u32[]{:S(2)}) copy-start(f32[64,4,1440]{2,0,1:T(8,128)} %all-reduce.8.cloned.1.call-done) | copy-start | bytes 4423684
  276.2 3.3 copy-start.2
Sparse Core Ops, SparseCore 0:
  11.6 46.8 all-reduce.5
  99.9 57.9 all-reduce.7
  214.6 57.9 all-reduce.9
where the time goes:
time: 343 us
  waiting for transfers between devices  152 us (44%)
  blocking collectives  100 us (29%)
  matrix products  38.3 us (11%)
  other arithmetic  24.3 us (7%)
  local copies, waits for them, and re-layouts  14 us (4%)
  between operations  13.9 us (4%)
    psum x2, waiting for transfers between devices, local(): cover = lax.psum(partial_cover, 'days')  116 us
    psum x2, blocking collectives, local(): gram, raw_pcs = lax.psum((partial_gram, partial_raw), 'space')  60 us
    psum x1, waiting for transfers between devices, local(): sums, counts = lax.psum((sums, counts), 'days')  36.2 us
    psum x1, blocking collectives, local(): pcs = lax.psum(partial_pcs, 'space')  28.5 us
    another operation x6, other arithmetic, local(): lower = jnp.linalg.cholesky(gram)  13 us
    psum x1, blocking collectives, local(): sums, counts = lax.psum((sums, counts), 'days')  11.5 us
    dot_general x2, matrix products, local(): jnp.einsum('dk,dlc->klc', pcs, weighted, precision=HIGH) / days_total  10.8 us
    dot_general x2, matrix products, local(): partial_raw = jnp.einsum('dlc,klc->dk', weighted, cover, precision=HIGH)  10.6 us
  transfers between devices with their start and end apart: 3, of which 3 were waited for; matrix products, arithmetic and copies ran while one was open for 0% of the time, Pallas kernels for 0%

commit v1 on v0

--- a/solution.py
+++ b/solution.py
@@ -38,7 +38,9 @@
     eofs = basis.astype(jnp.float32)
     for step_count in range(ITERS):
         partial_cover = jnp.einsum("dk,dlc->klc", pcs, weighted, precision=HIGH) / days_total
-        cover = lax.psum(partial_cover, "days")
+        cover = partial_cover
+        for hop in (1, 2):
+            cover = cover + lax.ppermute(cover, "days", [(dev, dev ^ hop) for dev in range(4)])
         partial_gram = self_gram(cover)
         partial_raw = jnp.einsum("dlc,klc->dk", weighted, cover, precision=HIGH)
         gram, raw_pcs = lax.psum((partial_gram, partial_raw), "space")

time: 343 us -> 354 us (1.032)
  blocking collectives: 100 us -> 109 us
  matrix products: 38.3 us -> 29.8 us
  waiting for transfers between devices: 152 us -> 160 us
  starting transfers between devices: 0.3 us -> 5.91 us
    ppermute x0 -> x4, waiting for transfers between devices: none -> 124 us  [local(): lax.ppermute(cover, 'days', [(dev, dev ^ hop) for dev in range(4)])]
    psum x2 -> x0, waiting for transfers between devices: 116 us -> none  [local(): cover = lax.psum(partial_cover, 'days')]
    psum x2, blocking collectives: 60 us -> 68.5 us  [local(): gram, raw_pcs = lax.psum((partial_gram, partial_raw), 'space')]
    ppermute x0 -> x4, starting transfers between devices: none -> 5.87 us  [local(): lax.ppermute(cover, 'days', [(dev, dev ^ hop) for dev in range(4)])]
    dot_general x2, matrix products: 10.6 us -> 6.39 us  [local(): partial_raw = jnp.einsum('dlc,klc->dk', weighted, cover, precision=HIGH)]
    psum x1 -> x0, local copies, waits for them, and re-layouts: 3.56 us -> none  [local(): cover = lax.psum(partial_cover, 'days')]
  transfers between devices with their start and end apart: 3 -> 5, of which waited for: 3 -> 5; matrix products, arithmetic and copies ran while one was open for 0% -> 0% of each run, Pallas kernels for 0% -> 0%
where the time goes in v1:
time: 354 us
  waiting for transfers between devices  160 us (45%)
  blocking collectives  109 us (31%)
  matrix products  29.8 us (8%)
  other arithmetic  25 us (7%)
  between operations  14.3 us (4%)
  local copies, waits for them, and re-layouts  10.5 us (3%)
  starting transfers between devices  5.91 us (2%)
    ppermute x4, waiting for transfers between devices, local(): lax.ppermute(cover, 'days', [(dev, dev ^ hop) for dev in range(4)])  124 us
    psum x2, blocking collectives, local(): gram, raw_pcs = lax.psum((partial_gram, partial_raw), 'space')  68.5 us
    psum x1, waiting for transfers between devices, local(): sums, counts = lax.psum((sums, counts), 'days')  36.2 us
    psum x1, blocking collectives, local(): pcs = lax.psum(partial_pcs, 'space')  28.5 us
    another operation x6, other arithmetic, local(): lower = jnp.linalg.cholesky(gram)  13 us
    psum x1, blocking collectives, local(): sums, counts = lax.psum((sums, counts), 'days')  11.5 us
    dot_general x2, matrix products, local(): jnp.einsum('dk,dlc->klc', pcs, weighted, precision=HIGH) / days_total  8.56 us
  transfers between devices with their start and end apart: 5, of which 5 were waited for; matrix products, arithmetic and copies ran while one was open for 0% of the time, Pallas kernels for 0%

profile of v1, /device:TPU:0, one launch (start us, length us, event | category | flops | bytes accessed | tf_op | source)
XLA Modules:
  0.0 353.8 jit_solution(15513263034136418239)
XLA Ops:
  7.3 3.1 fusion
  10.5 11.5 %psum.50 = f32[12]{0:T(128)S(1)} all-reduce(f32[12]{0:T(128)S(1)} %convert_reduce_fusion), channel_id=1, replica_groups=mesh['days'=4,'space'=8] {'days'}, use_global_device_ids=true, to_apply=%region_2.0 | all-reduce | flops 12 | bytes 96 | tf_op jit(solution)/shard_map/psum | solution.py:27
  22.2 36.2 %all-reduce.4.cloned.1.call-done = f32[12,4,1440]{2,0,1:T(8,128)} async-done(((f32[12,4,1440]{2,0,1:T(8,128)}), f32[12,4,1440]{2,0,1:T(8,128)}) %all-reduce.4.cloned.1.call-update) | async-done | bytes 276496 | tf_op jit(solution)/shard_map/psum | solution.py:27
  58.4 3.2 subtract_multiply_fusion
  61.6 1.9 copy-done.1
  63.5 2.4 convolution_bitcast_fusion.4
  65.9 28.5 %psum.51 = f32[160,64]{0,1:T(8,128)S(1)} all-reduce(f32[160,64]{0,1:T(8,128)S(1)} %convolution_bitcast_fusion.4), channel_id=1, replica_groups=mesh['days'=4,'space'=8] {'space'}, use_global_device_ids=true, to_apply=%region_3.0 | all-reduce | flops 10240 | bytes 81920 | tf_op jit(solution)/shard_map/psum | solution.py:37
  94.4 4.3 %convolution_multiply_fusion.1 = f32[64,4,1440]{2,0,1:T(8,128)S(1)} fusion(f32[160,4,1440]{2,0,1:T(8,128)} %copy-done.1, f32[160,64]{0,1:T(8,128)S(1)} %psum.51), kind=kOutput, calls=%fused_computation.2 | convolution fusion | flops 708157440 | bytes 5201920 | tf_op jit(solution)/shard_map/dk,dlc->klc/dot_general | solution.py:40
  98.7 1.5 collective-permute-start
  100.2 31.3 %collective-permute-done = f32[64,4,1440]{2,0,1:T(8,128)S(1)} collective-permute-done((f32[64,4,1440]{2,0,1:T(8,128)S(1)}, f32[64,4,1440]{2,0,1:T(8,128)S(1)}, u32[]{:S(2)}, u32[]{:S(2)}) %collective-permute-start) | collective-permute-done | bytes 1474592 | tf_op jit(solution)/shard_map/ppermute | solution.py:43
  131.8 1.4 collective-permute-start.1
  133.2 30.5 %collective-permute-done.1 = f32[64,4,1440]{2,0,1:T(8,128)S(1)} collective-permute-done((f32[64,4,1440]{2,0,1:T(8,128)S(1)}, f32[64,4,1440]{2,0,1:T(8,128)S(1)}, u32[]{:S(2)}, u32[]{:S(2)}) %collective-permute-start.1) | collective-permute-done | bytes 1474592 | tf_op jit(solution)/shard_map/ppermute | solution.py:43
  163.7 1.4 convolution_bitcast_fusion.6
  165.1 3.2 convolution_bitcast_fusion.1
  168.3 34.3 %all-reduce.1 = (f32[160,64]{1,0:T(8,128)S(1)}, f32[64,64]{0,1:T(8,128)S(1)}) all-reduce(f32[160,64]{1,0:T(8,128)S(1)} %convolution_bitcast_fusion.1, f32[64,64]{0,1:T(8,128)S(1)} %convolution_bitcast_fusion.6), channel_id=1, replica_groups=mesh['days'=4,'space'=8] {'space'}, use_global_device_ids=true, to_apply=%region_7.0 | all-reduce | flops 14336 | bytes 114688 | tf_op jit(solution)/shard_map/psum | solution.py:46
  202.8 5.8 %cholesky.44 = f32[64,64]{1,0:T(8,128)S(1)} custom-call(f32[64,64]{1,0:T(8,128)S(1)} %fusion.17), custom_call_target="Cholesky" | custom-call | tf_op jit(solution)/shard_map/jit(cholesky)/cholesky | solution.py:47
  210.0 4.9 %custom-call.10 = f32[1,64,64]{1,2,0:T(8,128)S(1)} custom-call(f32[1,64,64]{2,1,0:T(8,128)S(1)} %fusion.11), custom_call_target="InvertDiagBlocksLowerTriangular" | custom-call | tf_op jit(solution)/shard_map/triangular_solve/custom-call.0 | solution.py:49
  215.2 4.3 %convolution_multiply_fusion = f32[64,4,1440]{2,0,1:T(8,128)S(1)} fusion(f32[160,64,1]{0,1,2:T(8,128)S(1)} %convolution_bitcast_fusion.3, f32[160,4,1440]{2,0,1:T(8,128)} %copy-done.1), kind=kOutput, calls=%fused_computation.1 | convolution fusion | flops 708157440 | bytes 5201920 | tf_op jit(solution)/shard_map/dk,dlc->klc/dot_general | solution.py:40
  219.5 1.5 collective-permute-start.2
  221.0 31.3 %collective-permute-done.2 = f32[64,4,1440]{2,0,1:T(8,128)S(1)} collective-permute-done((f32[64,4,1440]{2,0,1:T(8,128)S(1)}, f32[64,4,1440]{2,0,1:T(8,128)S(1)}, u32[]{:S(2)}, u32[]{:S(2)}) %collective-permute-start.2) | collective-permute-done | bytes 1474592 | tf_op jit(solution)/shard_map/ppermute | solution.py:43
  252.5 1.4 collective-permute-start.3
  253.9 30.5 %collective-permute-done.3 = f32[64,4,1440]{2,0,1:T(8,128)S(1)} collective-permute-done((f32[64,4,1440]{2,0,1:T(8,128)S(1)}, f32[64,4,1440]{2,0,1:T(8,128)S(1)}, u32[]{:S(2)}, u32[]{:S(2)}) %collective-permute-start.3) | collective-permute-done | bytes 1474592 | tf_op jit(solution)/shard_map/ppermute | solution.py:43
  284.7 3.2 convolution_bitcast_fusion
  287.9 1.4 convolution_bitcast_fusion.5
  289.3 1.0 copy.19
  290.3 2.4 reshape.27
  292.6 34.2 %all-reduce = (f32[64,64]{0,1:T(8,128)S(1)}, f32[160,64]{1,0:T(8,128)S(1)}) all-reduce(f32[64,64]{0,1:T(8,128)S(1)} %convolution_bitcast_fusion.5, f32[160,64]{1,0:T(8,128)S(1)} %convolution_bitcast_fusion), channel_id=1, replica_groups=mesh['days'=4,'space'=8] {'space'}, use_global_device_ids=true, to_apply=%region_8.11 | all-reduce | flops 14336 | bytes 114688 | tf_op jit(solution)/shard_map/psum | solution.py:46
  327.0 5.8 %cholesky.55 = f32[64,64]{1,0:T(8,128)S(1)} custom-call(f32[64,64]{1,0:T(8,128)S(1)} %fusion.15), custom_call_target="Cholesky" | custom-call | tf_op jit(solution)/shard_map/jit(cholesky)/cholesky | solution.py:47
  334.1 4.9 %custom-call.8 = f32[1,64,64]{1,2,0:T(8,128)S(1)} custom-call(f32[1,64,64]{2,1,0:T(8,128)S(1)} %fusion.12), custom_call_target="InvertDiagBlocksLowerTriangular" | custom-call | tf_op jit(solution)/shard_map/triangular_solve | solution.py:12
  339.0 2.9 triangular_solve.34
  342.9 1.9 fusion.2
  344.8 2.2 copy.22
  (34 shorter events, 5.2 us)
Async XLA Ops:
  7.2 56.3 %copy-start = (bf16[64,4,1440]{2,1,0:T(4,128)(2,1)S(1)}, bf16[64,4,1440]{2,1,0:T(4,128)(2,1)}, u32[]{:S(2)}) copy-start(bf16[64,4,1440]{2,1,0:T(4,128)(2,1)} %param.12) | copy-start | bytes 2211844
  7.2 3.2 copy-start.5
  7.2 51.2 %copy-start.4 = (bf16[160,4,1440]{2,1,0:T(4,128)(2,1)S(1)}, bf16[160,4,1440]{2,1,0:T(4,128)(2,1)}, u32[]{:S(2)}) copy-start(bf16[160,4,1440]{2,1,0:T(4,128)(2,1)} %param.8) | copy-start | bytes 5529604
  7.2 14.8 %copy-start.7 = (f32[32]{0:T(128)S(1)}, f32[32]{0:T(128)}, u32[]{:S(2)}) copy-start(f32[32]{0:T(128)} %param.11) | copy-start | bytes 388
  7.2 14.8 %copy-start.6 = (s32[4]{0:T(128)S(1)}, s32[4]{0:T(128)}, u32[]{:S(2)}) copy-start(s32[4]{0:T(128)} %param.10) | copy-start | bytes 52
  7.2 51.2 %all-reduce.4.cloned.1.call-start = ((), (), s32[]{:S(2)}) async-start(), calls=%async_computation | async-start | bytes 786432 | tf_op jit(solution)/shard_map/psum | solution.py:27
  61.6 1.9 copy-start.1
  98.7 32.8 %collective-permute-start = (f32[64,4,1440]{2,0,1:T(8,128)S(1)}, f32[64,4,1440]{2,0,1:T(8,128)S(1)}, u32[]{:S(2)}, u32[]{:S(2)}) collective-permute-start(f32[64,4,1440]{2,0,1:T(8,128)S(1)} %convolution_multiply_fusion.1), channel_id=1, source_target_pairs={{0,8},{8,0},{16,24},{24,16},{1,9},{9,1},{17,25},{25,17},{2,10},{10... | collective-permute-start | bytes 4423688 | tf_op jit(solution)/shard_map/ppermute | solution.py:43
  131.5 33.6 %copy-start.2 = (f32[160,4,1440]{2,0,1:T(8,128)S(1)}, f32[160,4,1440]{2,0,1:T(8,128)}, u32[]{:S(2)}) copy-start(f32[160,4,1440]{2,0,1:T(8,128)} %copy-done.1) | copy-start | bytes 11059204
  131.8 32.0 %collective-permute-start.1 = (f32[64,4,1440]{2,0,1:T(8,128)S(1)}, f32[64,4,1440]{2,0,1:T(8,128)S(1)}, u32[]{:S(2)}, u32[]{:S(2)}) collective-permute-start(f32[64,4,1440]{2,0,1:T(8,128)S(1)} %add.36), channel_id=1, source_target_pairs={{0,16},{8,24},{16,0},{24,8},{1,17},{9,25},{17,1},{25,9},{2,18},{10... | collective-permute-start | bytes 4423688 | tf_op jit(solution)/shard_map/ppermute | solution.py:43
  219.5 32.8 %collective-permute-start.2 = (f32[64,4,1440]{2,0,1:T(8,128)S(1)}, f32[64,4,1440]{2,0,1:T(8,128)S(1)}, u32[]{:S(2)}, u32[]{:S(2)}) collective-permute-start(f32[64,4,1440]{2,0,1:T(8,128)S(1)} %convolution_multiply_fusion), channel_id=1, source_target_pairs={{0,8},{8,0},{16,24},{24,16},{1,9},{9,1},{17,25},{25,17},{2,10},{10... | collective-permute-start | bytes 4423688 | tf_op jit(solution)/shard_map/ppermute | solution.py:43
  252.5 32.2 %copy-start.3 = (f32[160,4,1440]{2,0,1:T(8,128)S(1)}, f32[160,4,1440]{2,0,1:T(8,128)}, u32[]{:S(2)}) copy-start(f32[160,4,1440]{2,0,1:T(8,128)} %copy-done.1) | copy-start | bytes 11059204
  252.5 31.9 %collective-permute-start.3 = (f32[64,4,1440]{2,0,1:T(8,128)S(1)}, f32[64,4,1440]{2,0,1:T(8,128)S(1)}, u32[]{:S(2)}, u32[]{:S(2)}) collective-permute-start(f32[64,4,1440]{2,0,1:T(8,128)S(1)} %add.38), channel_id=1, source_target_pairs={{0,16},{8,24},{16,0},{24,8},{1,17},{9,25},{17,1},{25,9},{2,18},{10... | collective-permute-start | bytes 4423688 | tf_op jit(solution)/shard_map/ppermute | solution.py:43
Sparse Core Ops, SparseCore 0:
  11.6 46.8 all-reduce.3
